TPU v7x, 32 devices: a whole 2x2x4 slice. The times are simulated.
32 devices in a mesh: trial: 4 (over y, x), rows: 2 (over core), cols: 4 (over z).
Axes of the slice: x: 2, y: 2, z: 4, core: 2. Of those that a mesh axis runs over, the one named last changes fastest.
Arguments:
- weight_gate: float32 [8192, 8192], P(('trial', 'rows'), 'cols'), parts along dimension 0, may hold values from -0.1875 to 0.1875
- moment_gate: float32 [8192, 8192], P(('trial', 'rows'), 'cols'), parts along dimension 0, may hold values from -6 to 6
- square_gate: float32 [8192, 8192], P(('trial', 'rows'), 'cols'), parts along dimension 0, may hold values from 0.1 to 10
- weight_up: float32 [8192, 8192], P(('trial', 'rows'), 'cols'), parts along dimension 0, may hold values from -0.1875 to 0.1875
- moment_up: float32 [8192, 8192], P(('trial', 'rows'), 'cols'), parts along dimension 0, may hold values from -6 to 6
- square_up: float32 [8192, 8192], P(('trial', 'rows'), 'cols'), parts along dimension 0, may hold values from 0.1 to 10
- norm_gain: float32 [8192], P(('trial', 'rows')), parts along dimension 0, may hold values from 0.25 to 1.75
Outputs:
- serving_gate: bfloat16 [8192, 8192], P('trial', 'cols'), parts along dimension 0
- serving_up: bfloat16 [8192, 8192], P('trial', 'cols'), parts along dimension 0
- column_gate: float32 [32768], P(('trial', 'cols')), parts along dimension 0
- column_up: float32 [32768], P(('trial', 'cols')), parts along dimension 0
There are 4 independent parts, one for each index of `trial`. A program takes and returns all parts, laid end to end along the dimension named above; each array names one. Nothing has to cross between parts.
All inputs are finite; a program needn't handle non-finite values. Where the computation divides by a largest or mean magnitude, that divisor is 1e-20 or more.
Results may differ from a plain program's by a relative error of at most 0.001.
Values may be sent and summed in bfloat16 or wider, within the bound.
A program may use at most 128 MiB of HBM per device.

v0:
```python
import functools

import jax
import jax.numpy as jnp
from jax import lax
from jax.experimental import pallas as pl
from jax.experimental.pallas import tpu as pltpu
from jax.sharding import PartitionSpec as P

learn_rate = 0.02
decay_rate = 0.05
tiny_value = 1e-08

LANES = 128
SLAB = 256
SLOTS = 8
MESH = pl.DeviceIdType.MESH


def exchange_kernel(
    n, wg, mg, sg, wu, mu, su, gain, out_g, out_u, col_g, col_u,
    w_buf, m_buf, s_buf, held, keep_scale, step_scale, parts,
    in_sem, part_send, part_recv, row_send, row_recv,
):
    rows, width = wg.shape
    slabs = width // SLAB
    steps = 2 * slabs
    chunk = min(rows, 256)
    me = lax.axis_index("rows")
    sources = ((wg, mg, sg), (wu, mu, su))
    outs = (out_g, out_u)
    cols = (col_g, col_u)
    buffers = (w_buf, m_buf, s_buf)

    def columns(j):
        return pl.ds(pl.multiple_of(j * SLAB, SLAB), SLAB)

    def loads(j, p):
        slot = lax.rem(2 * j + p, SLOTS)
        return [
            pltpu.make_async_copy(source.at[:, columns(j)], buffer.at[slot], in_sem.at[slot, i])
            for i, (source, buffer) in enumerate(zip(sources[p], buffers))
        ]

    def part_copy(j, p, k, owner):
        t = 2 * j + p
        return pltpu.make_async_remote_copy(
            src_ref=parts.at[t, owner],
            dst_ref=parts.at[t, owner],
            send_sem=part_send.at[t, k - 1],
            recv_sem=part_recv.at[t, k - 1],
            device_id={"rows": lax.rem(me + k, n)},
            device_id_type=MESH,
        )

    def row_copy(j, p, k, owner):
        t = 2 * j + p
        block = outs[p].at[pl.ds(pl.multiple_of(owner * rows, rows), rows), columns(j)]
        return pltpu.make_async_remote_copy(
            src_ref=block,
            dst_ref=block,
            send_sem=row_send.at[t, k - 1],
            recv_sem=row_recv.at[t, k - 1],
            device_id={"rows": lax.rem(me + k, n)},
            device_id_type=MESH,
        )

    def update(j, p):
        slot = lax.rem(2 * j + p, SLOTS)
        for copy in loads(j, p):
            copy.wait()

        def body(c, sums):
            at = pl.ds(pl.multiple_of(c * chunk, chunk), chunk)
            keep, scale = keep_scale[at, :], step_scale[at, :]
            new = []
            for i in range(SLAB // LANES):
                tile = pl.ds(i * LANES, LANES)
                square = s_buf[slot, at, tile]
                root = square * lax.rsqrt(square)
                value = w_buf[slot, at, tile] * keep - (m_buf[slot, at, tile] * scale) / (root + tiny_value)
                held[p, at, tile] = value
                new.append(sums[i] + jnp.sum(jnp.abs(value).reshape(chunk // 8, 8, LANES), axis=0))
            return tuple(new)

        zero = jnp.zeros((8, LANES), jnp.float32)
        sums = lax.fori_loop(0, rows // chunk, body, (zero,) * (SLAB // LANES))
        for i in range(SLAB // LANES):
            parts[2 * j + p, me, :, pl.ds(i * LANES, LANES)] = sums[i]

    def share_sums(j, p):
        for k in range(1, n):
            part_copy(j, p, k, me).start()

    def finish(j, p):
        t = 2 * j + p
        for k in range(1, n):
            part_copy(j, p, k, lax.rem(me + n - k, n)).wait_recv()
        total = parts[t, 0]
        for r in range(1, n):
            total = total + parts[t, r]
        column = jnp.sum(total, axis=0, keepdims=True) / (n * rows)
        cols[p][:, columns(j)] = column
        factor = 1.0 / column

        def body(c, carry):
            at = pl.ds(pl.multiple_of(c * chunk, chunk), chunk)
            to = pl.ds(pl.multiple_of(me * rows + c * chunk, chunk), chunk)
            outs[p][to, columns(j)] = (held[p, at, :] * factor).astype(jnp.bfloat16)
            return carry

        lax.fori_loop(0, rows // chunk, body, 0)

    def share_rows(j, p):
        for k in range(1, n):
            row_copy(j, p, k, me).start()

    ahead = min(SLOTS // 2, slabs)
    for j in range(ahead):
        for p in range(2):
            for copy in loads(j, p):
                copy.start()

    barrier = pltpu.get_barrier_semaphore()
    for k in range(1, n):
        pl.semaphore_signal(barrier, inc=1, device_id={"rows": lax.rem(me + k, n)}, device_id_type=MESH)

    for r in range(rows // LANES):
        spread = jnp.broadcast_to(gain[r : r + 1, :], (LANES, LANES)).T
        at = pl.ds(r * LANES, LANES)
        keep_scale[at, :] = spread * (1.0 - learn_rate * decay_rate)
        step_scale[at, :] = spread * learn_rate

    pl.semaphore_wait(barrier, n - 1)

    def refill(j, p):
        @pl.when(j + ahead < slabs)
        def _():
            for copy in loads(j + ahead, p):
                copy.start()

    def step(j, carry):
        update(j, 0)
        share_sums(j, 0)
        refill(j, 0)

        @pl.when(j > 0)
        def _():
            finish(j - 1, 1)
            share_rows(j - 1, 1)

        update(j, 1)
        share_sums(j, 1)
        refill(j, 1)
        finish(j, 0)
        share_rows(j, 0)
        return carry

    lax.fori_loop(0, slabs, step, 0)
    finish(slabs - 1, 1)
    share_rows(slabs - 1, 1)

    def drain(j, carry):
        for p in range(2):
            for k in range(1, n):
                part_copy(j, p, k, me).wait_send()
                row_copy(j, p, k, me).wait_send()
                row_copy(j, p, k, lax.rem(me + n - k, n)).wait_recv()
        return carry

    lax.fori_loop(0, slabs, drain, 0)


def store_kernel(pieces, gate, up, col_g, col_u, out_g, out_u, out_cg, out_cu, sem, col_sem):
    height = gate.shape[0] // pieces
    copies = []
    for p, (source, target) in enumerate(((gate, out_g), (up, out_u))):
        for i in range(pieces):
            at = pl.ds(i * height, height)
            copies.append(pltpu.make_async_copy(source.at[at, :], target.at[at, :], sem.at[p, i]))
    copies.append(pltpu.make_async_copy(col_g, out_cg, col_sem.at[0]))
    copies.append(pltpu.make_async_copy(col_u, out_cu, col_sem.at[1]))
    for copy in copies:
        copy.start()
    for copy in copies:
        copy.wait()


def solution(mesh):
    n = mesh.shape["rows"]

    def shards(weight_gate, moment_gate, square_gate, weight_up, moment_up, square_up, norm_gain):
        rows, width = weight_gate.shape
        steps = 2 * (width // SLAB)
        any_space = pl.BlockSpec(memory_space=pl.ANY)
        in_vmem = pl.BlockSpec(memory_space=pltpu.VMEM)
        shapes = (
            ((n * rows, width), jnp.bfloat16),
            ((n * rows, width), jnp.bfloat16),
            ((1, width), jnp.float32),
            ((1, width), jnp.float32),
        )
        dma = pltpu.SemaphoreType.DMA
        moved = pl.pallas_call(
            functools.partial(exchange_kernel, n),
            out_shape=tuple(pltpu.VMEM(*shape) for shape in shapes),
            in_specs=[any_space] * 6 + [in_vmem],
            out_specs=[in_vmem] * 4,
            scratch_shapes=[
                pltpu.VMEM((SLOTS, rows, SLAB), jnp.float32),
                pltpu.VMEM((SLOTS, rows, SLAB), jnp.float32),
                pltpu.VMEM((SLOTS, rows, SLAB), jnp.float32),
                pltpu.VMEM((2, rows, SLAB), jnp.float32),
                pltpu.VMEM((rows, LANES), jnp.float32),
                pltpu.VMEM((rows, LANES), jnp.float32),
                pltpu.VMEM((steps, n, 8, SLAB), jnp.float32),
                dma((SLOTS, 3)),
                dma((steps, max(n - 1, 1))),
                dma((steps, max(n - 1, 1))),
                dma((steps, max(n - 1, 1))),
                dma((steps, max(n - 1, 1))),
            ],
            compiler_params=pltpu.CompilerParams(
                collective_id=0, has_side_effects=True, vmem_limit_bytes=36 * 1024 * 1024
            ),
            name="exchange",
        )(
            weight_gate, moment_gate, square_gate, weight_up, moment_up, square_up,
            norm_gain.reshape(rows // LANES, LANES),
        )
        pieces = 4
        gate, up, col_g, col_u = pl.pallas_call(
            functools.partial(store_kernel, pieces),
            out_shape=tuple(jax.ShapeDtypeStruct(*shape) for shape in shapes),
            in_specs=[in_vmem] * 4,
            out_specs=[any_space] * 4,
            scratch_shapes=[dma((2, pieces)), dma((2,))],
            compiler_params=pltpu.CompilerParams(vmem_limit_bytes=1024 * 1024),
            name="store",
        )(*moved)
        return gate, up, col_g.reshape(width), col_u.reshape(width)

    held = P(("trial", "rows"), "cols")
    return jax.shard_map(
        shards,
        mesh=mesh,
        in_specs=(held,) * 6 + (P(("trial", "rows")),),
        out_specs=(P("trial", "cols"), P("trial", "cols"), P(("trial", "cols")), P(("trial", "cols"))),
        check_vma=False,
    )
```

profile of v0, /device:TPU:3, one launch (start us, length us, event | category | flops | bytes accessed | tf_op | source)
XLA Modules:
  0.0 27.4 jit_solution(16764290825659072984)
XLA Ops:
  0.6 0.0 copy-start
  0.6 0.7 %copy-done = f32[1024]{0:T(1024)S(1)} copy-done((f32[1024]{0:T(1024)S(1)}, f32[1024]{0:T(1024)}, u32[]{:S(2)}) %copy-start) | copy-done | bytes 4120
  1.3 20.1 %exchange.1 = (bf16[2048,2048]{1,0:T(8,128)(2,1)S(1)}, bf16[2048,2048]{1,0:T(8,128)(2,1)S(1)}, f32[1,2048]{1,0:T(1,128)S(1)}, f32[1,2048]{1,0:T(1,128)S(1)}) custom-call(f32[1024,2048]{1,0:T(8,128)} %wg.1, f32[1024,2048]{1,0:T(8,128)} %mg.1, f32[1024,2048]{1,0:T(8,128)} %sg.1, f32[1024,2048]{1,0:T(8,128)} %wu.1, f32[1024,2048]{1,0:T(8,128)} %mu.1, ...), custom_call_target="tpu_custom_call" | custom-call | tf_op jit(solution)/shard_map/exchange/pallas_call | solution.py:204
  21.5 6.0 %store.1 = (bf16[2048,2048]{1,0:T(8,128)(2,1)}, bf16[2048,2048]{1,0:T(8,128)(2,1)}, f32[1,2048]{1,0:T(1,128)}, f32[1,2048]{1,0:T(1,128)}) custom-call(bf16[2048,2048]{1,0:T(8,128)(2,1)S(1)} %get-tuple-element.12.gate, bf16[2048,2048]{1,0:T(8,128)(2,1)S(1)} %get-tuple-element.13.up, f32[1,2048]{1,0:T(1,128)S(1)} %get-tuple-element.14.col_g, ...), custom_call_target="tpu_custom_call" | custom-call | tf_op jit(solution)/shard_map/store/pallas_call | solution.py:232
Async XLA Ops:
  0.6 0.7 %copy-start = (f32[1024]{0:T(1024)S(1)}, f32[1024]{0:T(1024)}, u32[]{:S(2)}) copy-start(f32[1024]{0:T(1024)} %param.13) | copy-start | bytes 12292
where the time goes:
time: 27.6 us; the launch traced here: 27.4 us
  Pallas kernels  26.1 us (95%)
  local copies, waits for them, and re-layouts  0.68 us (2%)
  between operations  0.65 us (2%)
    pallas_call x1, Pallas kernels, shards(): pl.pallas_call(functools.partial(exchange_kernel, n), out_shape=tuple((pl...  20.1 us
    pallas_call x1, Pallas kernels, shards(): pl.pallas_call(functools.partial(store_kernel, pieces), out_shape=tuple((...  5.95 us
    unnamed x2, local copies, waits for them, and re-layouts  0.68 us

commit v1 on v0

v1 whole, which is shorter than its diff:
```python
import functools

import jax
import jax.numpy as jnp
from jax import lax
from jax.experimental import pallas as pl
from jax.experimental.pallas import tpu as pltpu
from jax.sharding import PartitionSpec as P

learn_rate = 0.02
decay_rate = 0.05
tiny_value = 1e-08

LANES = 128
SLAB = 256
SLOTS = 8
REST = 3
MESH = pl.DeviceIdType.MESH


def unit_of(t):
    return t // 2, t % 2


def exchange_kernel(
    n, wg, mg, sg, wu, mu, su, gain_hbm, out_g, out_u, col_g, col_u, rest,
    w_buf, m_buf, s_buf, held, gain, keep_scale, step_scale, parts,
    in_sem, part_send, part_recv, row_send, row_recv, gain_sem,
):
    rows, width = wg.shape
    units = 2 * (width // SLAB)
    bulk = units - REST
    chunk = min(rows, 256)
    me = lax.axis_index("rows")
    sources = ((wg, mg, sg), (wu, mu, su))
    outs = (out_g, out_u)
    cols = (col_g, col_u)
    buffers = (w_buf, m_buf, s_buf)

    def columns(j):
        return pl.ds(pl.multiple_of(j * SLAB, SLAB), SLAB)

    def loads(j, p):
        slot = lax.rem(2 * j + p, SLOTS)
        return [
            pltpu.make_async_copy(source.at[:, columns(j)], buffer.at[slot], in_sem.at[slot, i])
            for i, (source, buffer) in enumerate(zip(sources[p], buffers))
        ]

    def part_copy(j, p, k, owner):
        t = 2 * j + p
        return pltpu.make_async_remote_copy(
            src_ref=parts.at[t, owner],
            dst_ref=parts.at[t, owner],
            send_sem=part_send.at[t, k - 1],
            recv_sem=part_recv.at[t, k - 1],
            device_id={"rows": lax.rem(me + k, n)},
            device_id_type=MESH,
        )

    def row_copy(j, p, k, owner):
        t = 2 * j + p
        block = outs[p].at[pl.ds(pl.multiple_of(owner * rows, rows), rows), columns(j)]
        return pltpu.make_async_remote_copy(
            src_ref=block,
            dst_ref=block,
            send_sem=row_send.at[t, k - 1],
            recv_sem=row_recv.at[t, k - 1],
            device_id={"rows": lax.rem(me + k, n)},
            device_id_type=MESH,
        )

    zero = jnp.zeros((8, LANES), jnp.float32)

    def update(j, p, keep_value):
        slot = lax.rem(2 * j + p, SLOTS)
        for copy in loads(j, p):
            copy.wait()

        def body(c, sums):
            at = pl.ds(pl.multiple_of(c * chunk, chunk), chunk)
            keep, scale = keep_scale[at, :], step_scale[at, :]
            new = []
            for i in range(SLAB // LANES):
                tile = pl.ds(i * LANES, LANES)
                square = s_buf[slot, at, tile]
                root = square * lax.rsqrt(square)
                value = w_buf[slot, at, tile] * keep - (m_buf[slot, at, tile] * scale) / (root + tiny_value)
                keep_value(at, tile, value)
                new.append(sums[i] + jnp.sum(jnp.abs(value).reshape(chunk // 8, 8, LANES), axis=0))
            return tuple(new)

        return lax.fori_loop(0, rows // chunk, body, (zero,) * (SLAB // LANES))

    def update_bulk(j, p):
        def keep_value(at, tile, value):
            held[p, at, tile] = value

        sums = update(j, p, keep_value)
        for i in range(SLAB // LANES):
            parts[2 * j + p, me, :, pl.ds(i * LANES, LANES)] = sums[i]
        for k in range(1, n):
            part_copy(j, p, k, me).start()

    def update_rest(j, p, u):
        def keep_value(at, tile, value):
            rest[u, at, tile] = value

        sums = update(j, p, keep_value)
        for i in range(SLAB // LANES):
            rest[u, pl.ds(rows, 8), pl.ds(i * LANES, LANES)] = sums[i]

    def finish(j, p):
        t = 2 * j + p
        for k in range(1, n):
            part_copy(j, p, k, lax.rem(me + n - k, n)).wait_recv()
        total = parts[t, 0]
        for r in range(1, n):
            total = total + parts[t, r]
        column = jnp.sum(total, axis=0, keepdims=True) / (n * rows)
        cols[p][:, columns(j)] = column
        factor = 1.0 / column

        def body(c, carry):
            at = pl.ds(pl.multiple_of(c * chunk, chunk), chunk)
            to = pl.ds(pl.multiple_of(me * rows + c * chunk, chunk), chunk)
            outs[p][to, columns(j)] = (held[p, at, :] * factor).astype(jnp.bfloat16)
            return carry

        lax.fori_loop(0, rows // chunk, body, 0)
        for k in range(1, n):
            row_copy(j, p, k, me).start()

    gain_copy = pltpu.make_async_copy(gain_hbm, gain, gain_sem)
    gain_copy.start()
    ahead = min(SLOTS, units)

    def begin(j, carry):
        for p in range(2):
            for copy in loads(j, p):
                copy.start()
        return carry

    lax.fori_loop(0, ahead // 2, begin, 0)

    barrier = pltpu.get_barrier_semaphore()
    for k in range(1, n):
        pl.semaphore_signal(barrier, inc=1, device_id={"rows": lax.rem(me + k, n)}, device_id_type=MESH)

    gain_copy.wait()
    for r in range(rows // LANES):
        spread = jnp.broadcast_to(gain[r : r + 1, :], (LANES, LANES)).T
        at = pl.ds(r * LANES, LANES)
        keep_scale[at, :] = spread * (1.0 - learn_rate * decay_rate)
        step_scale[at, :] = spread * learn_rate

    pl.semaphore_wait(barrier, n - 1)

    def refill(j, p):
        @pl.when(2 * j + p + ahead < units)
        def _():
            for copy in loads(j + ahead // 2, p):
                copy.start()

    def step(j, carry):
        update_bulk(j, 0)
        refill(j, 0)

        @pl.when(j > 0)
        def _():
            finish(j - 1, 1)

        update_bulk(j, 1)
        refill(j, 1)
        finish(j, 0)
        return carry

    lax.fori_loop(0, bulk // 2, step, 0)
    waiting = [bulk // 2 * 2 - 1]
    if bulk % 2:
        update_bulk(*unit_of(bulk - 1))
        finish(*unit_of(waiting.pop()))
        waiting.append(bulk - 1)
    for t in range(bulk, units):
        update_rest(*unit_of(t), t - bulk)
        if waiting:
            finish(*unit_of(waiting.pop()))

    def drained(j, p):
        for k in range(1, n):
            part_copy(j, p, k, me).wait_send()
            row_copy(j, p, k, me).wait_send()
            row_copy(j, p, k, lax.rem(me + n - k, n)).wait_recv()

    def drain(j, carry):
        for p in range(2):
            drained(j, p)
        return carry

    lax.fori_loop(0, bulk // 2, drain, 0)
    if bulk % 2:
        drained(*unit_of(bulk - 1))


def store_kernel(pieces, ends, gate, up, out_g, out_u, sem):
    height = gate.shape[0] // pieces
    copies = []
    for p, (source, target) in enumerate(((gate, out_g), (up, out_u))):
        for i in range(pieces):
            at = (pl.ds(i * height, height), pl.ds(0, ends[p]))
            copies.append(pltpu.make_async_copy(source.at[at], target.at[at], sem.at[p, i]))
    for copy in copies:
        copy.start()
    for copy in copies:
        copy.wait()


def rest_kernel(n, bulk, *refs):
    own, peers = refs[0], refs[1:n]
    col_g, col_u, _, _, out_g, out_u, out_cg, out_cu, block, column, sem, col_sem = refs[n:]
    rows = own.shape[1] - 8
    chunk = min(rows, 256)
    me = lax.axis_index("rows")
    outs = (out_g, out_u)
    copies = []
    for u in range(REST):
        j, p = unit_of(bulk + u)
        at_columns = pl.ds(j * SLAB, SLAB)
        tail = pl.ds(rows, 8)
        total = own[u, tail, :]
        for peer in peers:
            total = total + peer[u, tail, :]
        mean = jnp.sum(total, axis=0, keepdims=True) / (n * rows)
        (col_g, col_u)[p][:, at_columns] = mean
        factor = 1.0 / mean
        for k, source in enumerate((own, *peers)):
            owner = lax.rem(me + n - k, n)

            def body(c, carry):
                at = pl.ds(pl.multiple_of(c * chunk, chunk), chunk)
                to = pl.ds(pl.multiple_of(owner * rows + c * chunk, chunk), chunk)
                block[u, to, :] = (source[u, at, :] * factor).astype(jnp.bfloat16)
                return carry

            lax.fori_loop(0, rows // chunk, body, 0)
            to = pl.ds(pl.multiple_of(owner * rows, rows), rows)
            copies.append(pltpu.make_async_copy(block.at[u, to], outs[p].at[to, at_columns], sem.at[u, k]))
            copies[-1].start()
    for p in range(2):
        copies.append(pltpu.make_async_copy((col_g, col_u)[p], (out_cg, out_cu)[p], col_sem.at[p]))
        copies[-1].start()
    for copy in copies:
        copy.wait()


def solution(mesh):
    n = mesh.shape["rows"]

    def shards(weight_gate, moment_gate, square_gate, weight_up, moment_up, square_up, norm_gain):
        rows, width = weight_gate.shape
        units = 2 * (width // SLAB)
        bulk = units - REST
        peers = max(n - 1, 1)
        any_space = pl.BlockSpec(memory_space=pl.ANY)
        in_vmem = pl.BlockSpec(memory_space=pltpu.VMEM)
        full = ((n * rows, width), jnp.bfloat16)
        column = ((1, width), jnp.float32)
        dma = pltpu.SemaphoreType.DMA
        gate, up, col_g, col_u, rest = pl.pallas_call(
            functools.partial(exchange_kernel, n),
            out_shape=tuple(
                pltpu.VMEM(*shape) for shape in (full, full, column, column, ((REST, rows + 8, SLAB), jnp.float32))
            ),
            in_specs=[any_space] * 6 + [pl.BlockSpec(memory_space=pltpu.HBM)],
            out_specs=[in_vmem] * 5,
            scratch_shapes=[
                pltpu.VMEM((SLOTS, rows, SLAB), jnp.float32),
                pltpu.VMEM((SLOTS, rows, SLAB), jnp.float32),
                pltpu.VMEM((SLOTS, rows, SLAB), jnp.float32),
                pltpu.VMEM((2, rows, SLAB), jnp.float32),
                pltpu.VMEM((rows // LANES, LANES), jnp.float32),
                pltpu.VMEM((rows, LANES), jnp.float32),
                pltpu.VMEM((rows, LANES), jnp.float32),
                pltpu.VMEM((bulk, n, 8, SLAB), jnp.float32),
                dma((SLOTS, 3)),
                dma((bulk, peers)),
                dma((bulk, peers)),
                dma((bulk, peers)),
                dma((bulk, peers)),
                dma,
            ],
            compiler_params=pltpu.CompilerParams(
                collective_id=0, has_side_effects=True, vmem_limit_bytes=36 * 1024 * 1024
            ),
            name="exchange",
        )(
            weight_gate, moment_gate, square_gate, weight_up, moment_up, square_up,
            norm_gain.reshape(rows // LANES, LANES),
        )
        others = [
            lax.ppermute(rest, "rows", [(i, (i + k) % n) for i in range(n)]) for k in range(1, n)
        ]
        pieces = 4
        ends = ((bulk + 1) // 2 * SLAB, bulk // 2 * SLAB)
        out_g, out_u = pl.pallas_call(
            functools.partial(store_kernel, pieces, ends),
            out_shape=(jax.ShapeDtypeStruct(*full),) * 2,
            in_specs=[in_vmem] * 2,
            out_specs=[any_space] * 2,
            scratch_shapes=[dma((2, pieces))],
            compiler_params=pltpu.CompilerParams(vmem_limit_bytes=1024 * 1024),
            cost_estimate=pl.CostEstimate(flops=200_000_000, bytes_accessed=4 * n * rows * width, transcendentals=0),
            name="store",
        )(gate, up)
        first = n + 2
        out_g, out_u, out_cg, out_cu = pl.pallas_call(
            functools.partial(rest_kernel, n, bulk),
            out_shape=(jax.ShapeDtypeStruct(*full),) * 2 + (jax.ShapeDtypeStruct(*column),) * 2,
            in_specs=[in_vmem] * first + [any_space] * 2,
            out_specs=[any_space] * 4,
            input_output_aliases={first: 0, first + 1: 1},
            scratch_shapes=[
                pltpu.VMEM((REST, n * rows, SLAB), jnp.bfloat16),
                pltpu.VMEM((1, SLAB), jnp.float32),
                dma((REST, n)),
                dma((2,)),
            ],
            compiler_params=pltpu.CompilerParams(vmem_limit_bytes=8 * 1024 * 1024),
            name="rest",
        )(rest, *others, col_g, col_u, out_g, out_u)
        return out_g, out_u, out_cg.reshape(width), out_cu.reshape(width)

    held = P(("trial", "rows"), "cols")
    return jax.shard_map(
        shards,
        mesh=mesh,
        in_specs=(held,) * 6 + (P(("trial", "rows")),),
        out_specs=(P("trial", "cols"), P("trial", "cols"), P(("trial", "cols")), P(("trial", "cols"))),
        check_vma=False,
    )
```

time: 27.6 us -> 25.9 us (0.938)
  Pallas kernels: 26.1 us -> 24.3 us
  local copies, waits for them, and re-layouts: 0.68 us -> 0 us
  starting transfers between devices: 0 us -> 0.47 us
  waiting for transfers between devices: 0 us -> 0.32 us
    pallas_call x1, Pallas kernels: 20.1 us -> 17.5 us  [shards(): pl.pallas_call(functools.partial(exchange_kernel, n), out_shape=tuple((pl...]
    pallas_call x1 -> x2, Pallas kernels: 5.95 us -> 6.81 us  [the longest x1 4.99 us: shards(): pl.pallas_call(functools.partial(store_kernel, pieces, ends), out_shape=(...]
    unnamed x2 -> x0, local copies, waits for them, and re-layouts: 0.68 us -> none
    ppermute x0 -> x1, starting transfers between devices: none -> 0.47 us  [shards(): lax.ppermute(rest, 'rows', [(i, (i + k) % n) for i in range(n)])]
    ppermute x0 -> x1, waiting for transfers between devices: none -> 0.32 us  [shards(): lax.ppermute(rest, 'rows', [(i, (i + k) % n) for i in range(n)])]
  transfers between devices with their start and end apart: 0 -> 1, of which waited for: 0 -> 1; matrix products, arithmetic and copies ran while one was open for 0% -> 0% of each run, Pallas kernels for 0% -> 19%
where the time goes in v1:
time: 25.9 us; the launch traced here: 25.7 us
  Pallas kernels  24.3 us (94%)
  between operations  0.65 us (3%)
  starting transfers between devices  0.47 us (2%)
  waiting for transfers between devices  0.32 us (1%)
    pallas_call x1, Pallas kernels, shards(): pl.pallas_call(functools.partial(exchange_kernel, n), out_shape=tuple((pl...  17.5 us
    pallas_call x1, Pallas kernels, shards(): pl.pallas_call(functools.partial(store_kernel, pieces, ends), out_shape=(...  4.99 us
    pallas_call x1, Pallas kernels, shards(): pl.pallas_call(functools.partial(rest_kernel, n, bulk), out_shape=(jax.Sh...  1.82 us
  transfers between devices with their start and end apart: 1, of which 1 were waited for; matrix products, arithmetic and copies ran while one was open for 0% of the time, Pallas kernels for 19%

profile of v1, /device:TPU:3, one launch (start us, length us, event | category | flops | bytes accessed | tf_op | source)
XLA Modules:
  0.0 25.7 jit_solution(3380288425406340136)
XLA Ops:
  0.6 17.5 %exchange.1 = (bf16[2048,2048]{1,0:T(8,128)(2,1)S(1)}, bf16[2048,2048]{1,0:T(8,128)(2,1)S(1)}, f32[1,2048]{1,0:T(1,128)S(1)}, f32[1,2048]{1,0:T(1,128)S(1)}, f32[3,1032,256]{2,1,0:T(8,128)S(1)}) custom-call(f32[1024,2048]{1,0:T(8,128)} %wg.1, f32[1024,2048]{1,0:T(8,128)} %mg.1, f32[1024,2048]{1,0:T(8,128)} %sg.1, f32[1024,2048]{1,0:T(8,128)} %wu.1, ...), custom_call_target="tpu_custom_call" | custom-call | tf_op jit(solution)/shard_map/exchange/pallas_call | solution.py:269
  18.1 0.5 %collective-permute-start = (f32[3,1032,256]{2,1,0:T(8,128)S(1)}, f32[3,1032,256]{2,1,0:T(8,128)S(1)}, u32[]{:S(2)}, u32[]{:S(2)}) collective-permute-start(f32[3,1032,256]{2,1,0:T(8,128)S(1)} %get-tuple-element.15.refs_0_), channel_id=1, source_target_pairs={{0,4},{4,0},{1,5},{5,1},{2,6},{6,2},{3,7},{7,3},{8,12},{12,8},{9,1... | collective-permute-start | bytes 9510920 | tf_op jit(solution)/shard_map/ppermute | solution.py:301
  18.6 5.0 %store.1 = (bf16[2048,2048]{1,0:T(8,128)(2,1)}, bf16[2048,2048]{1,0:T(8,128)(2,1)}) custom-call(bf16[2048,2048]{1,0:T(8,128)(2,1)S(1)} %get-tuple-element.18.gate, bf16[2048,2048]{1,0:T(8,128)(2,1)S(1)} %get-tuple-element.19.up), custom_call_target="tpu_custom_call" | custom-call | flops 200000000 | bytes 16777216 | tf_op jit(solution)/shard_map/store/pallas_call | solution.py:305
  23.6 0.3 %collective-permute-done.refs_1_ = f32[3,1032,256]{2,1,0:T(8,128)S(1)} collective-permute-done((f32[3,1032,256]{2,1,0:T(8,128)S(1)}, f32[3,1032,256]{2,1,0:T(8,128)S(1)}, u32[]{:S(2)}, u32[]{:S(2)}) %collective-permute-start) | collective-permute-done | bytes 3170336 | tf_op jit(solution)/shard_map/ppermute | solution.py:301
  23.9 1.8 %rest.1 = (bf16[2048,2048]{1,0:T(8,128)(2,1)}, bf16[2048,2048]{1,0:T(8,128)(2,1)}, f32[1,2048]{1,0:T(1,128)}, f32[1,2048]{1,0:T(1,128)}) custom-call(f32[3,1032,256]{2,1,0:T(8,128)S(1)} %get-tuple-element.15.refs_0_, f32[3,1032,256]{2,1,0:T(8,128)S(1)} %collective-permute-done.refs_1_, ...), custom_call_target="tpu_custom_call", output_to_operand_aliasing={{0}: (4, {}), {1}: (5, {})} | custom-call | tf_op jit(solution)/shard_map/rest/pallas_call | solution.py:316
Async XLA Ops:
  18.1 5.8 %collective-permute-start = (f32[3,1032,256]{2,1,0:T(8,128)S(1)}, f32[3,1032,256]{2,1,0:T(8,128)S(1)}, u32[]{:S(2)}, u32[]{:S(2)}) collective-permute-start(f32[3,1032,256]{2,1,0:T(8,128)S(1)} %get-tuple-element.15.refs_0_), channel_id=1, source_target_pairs={{0,4},{4,0},{1,5},{5,1},{2,6},{6,2},{3,7},{7,3},{8,12},{12,8},{9,1... | collective-permute-start | bytes 9510920 | tf_op jit(solution)/shard_map/ppermute | solution.py:301

commit v2 on v1

v2 whole, which is shorter than its diff:
```python
import functools

import jax
import jax.numpy as jnp
from jax import lax
from jax.experimental import pallas as pl
from jax.experimental.pallas import tpu as pltpu
from jax.sharding import PartitionSpec as P

learn_rate = 0.02
decay_rate = 0.05
tiny_value = 1e-08

LANES = 128
SLAB = 256
SLOTS = 4
RING = 4
READY = 1
REST = 2
MESH = pl.DeviceIdType.MESH


def unit_of(t):
    return t // 2, t % 2


def exchange_kernel(
    n, wg, mg, sg, wu, mu, su, gain_hbm, out_g, out_u, col_g, col_u, ready, rest,
    buf, held, gain, keep_scale, step_scale, parts,
    in_sem, part_send, part_recv, row_send, row_recv, gain_sem, piece_sem,
):
    rows, width = wg.shape
    units = 2 * (width // SLAB)
    whole = units - REST
    bulk = whole - READY
    chunk = min(rows, 256)
    me = lax.axis_index("rows")
    sources = ((wg, mg, sg), (wu, mu, su))
    outs = (out_g, out_u)
    cols = (col_g, col_u)

    def columns(j):
        return pl.ds(pl.multiple_of(j * SLAB, SLAB), SLAB)

    def loads(j, p):
        slot = lax.rem(2 * j + p, SLOTS)
        return [
            pltpu.make_async_copy(source.at[:, columns(j)], buf.at[slot, i], in_sem.at[slot])
            for i, source in enumerate(sources[p])
        ]

    def loaded(slot):
        pltpu.make_async_copy(buf.at[slot], buf.at[slot], in_sem.at[slot]).wait()

    def piece_loads(c):
        j, p = unit_of(units - 1)
        at = pl.ds(pl.multiple_of(c * chunk, chunk), chunk)
        return [
            pltpu.make_async_copy(source.at[at, columns(j)], buf.at[(units - 1) % SLOTS, i, at], piece_sem.at[c])
            for i, source in enumerate(sources[p])
        ]

    def piece_loaded(c):
        block = buf.at[(units - 1) % SLOTS, :, pl.ds(pl.multiple_of(c * chunk, chunk), chunk)]
        pltpu.make_async_copy(block, block, piece_sem.at[c]).wait()

    def part_copy(j, p, k, owner):
        t = 2 * j + p
        return pltpu.make_async_remote_copy(
            src_ref=parts.at[t, owner],
            dst_ref=parts.at[t, owner],
            send_sem=part_send.at[lax.rem(t, RING), k - 1],
            recv_sem=part_recv.at[lax.rem(t, RING), k - 1],
            device_id={"rows": lax.rem(me + k, n)},
            device_id_type=MESH,
        )

    def row_copy(p, k, owner, at_columns):
        block = outs[p].at[pl.ds(pl.multiple_of(owner * rows, rows), rows), at_columns]
        return pltpu.make_async_remote_copy(
            src_ref=block,
            dst_ref=block,
            send_sem=row_send.at[p, k - 1],
            recv_sem=row_recv.at[p, k - 1],
            device_id={"rows": lax.rem(me + k, n)},
            device_id_type=MESH,
        )

    zero = jnp.zeros((8, LANES), jnp.float32)

    def update(j, p, keep_value, pieces=False):
        slot = lax.rem(2 * j + p, SLOTS)
        if not pieces:
            loaded(slot)

        def body(c, sums):
            if pieces:
                piece_loaded(c)
            at = pl.ds(pl.multiple_of(c * chunk, chunk), chunk)
            keep, scale = keep_scale[at, :], step_scale[at, :]
            new = []
            for i in range(SLAB // LANES):
                tile = pl.ds(i * LANES, LANES)
                square = buf[slot, 2, at, tile]
                root = square * lax.rsqrt(square)
                value = buf[slot, 0, at, tile] * keep - (buf[slot, 1, at, tile] * scale) / (root + tiny_value)
                keep_value(at, tile, value)
                new.append(sums[i] + jnp.sum(jnp.abs(value).reshape(chunk // 8, 8, LANES), axis=0))
            return tuple(new)

        return lax.fori_loop(0, rows // chunk, body, (zero,) * (SLAB // LANES))

    def update_shared(j, p):
        def keep_value(at, tile, value):
            held[p, at, tile] = value

        sums = update(j, p, keep_value)
        for i in range(SLAB // LANES):
            parts[2 * j + p, me, :, pl.ds(i * LANES, LANES)] = sums[i]
        for k in range(1, n):
            part_copy(j, p, k, me).start()

    def update_rest(j, p, u):
        def keep_value(at, tile, value):
            rest[u, at, tile] = value

        sums = update(j, p, keep_value, pieces=2 * j + p == units - 1)
        for i in range(SLAB // LANES):
            rest[u, pl.ds(rows, 8), pl.ds(i * LANES, LANES)] = sums[i]

    def factor_of(j, p):
        t = 2 * j + p
        for k in range(1, n):
            part_copy(j, p, k, lax.rem(me + n - k, n)).wait_recv()
            part_copy(j, p, k, me).wait_send()
        total = parts[t, 0]
        for r in range(1, n):
            total = total + parts[t, r]
        column = jnp.sum(total, axis=0, keepdims=True) / (n * rows)
        cols[p][:, columns(j)] = column
        return 1.0 / column

    def finish_ready(j, p):
        factor = factor_of(j, p)

        def body(c, carry):
            at = pl.ds(pl.multiple_of(c * chunk, chunk), chunk)
            ready[2 * j + p - bulk, at, :] = (held[p, at, :] * factor).astype(jnp.bfloat16)
            return carry

        lax.fori_loop(0, rows // chunk, body, 0)

    def finish(j, p):
        factor = factor_of(j, p)

        def body(c, carry):
            at = pl.ds(pl.multiple_of(c * chunk, chunk), chunk)
            to = pl.ds(pl.multiple_of(me * rows + c * chunk, chunk), chunk)
            outs[p][to, columns(j)] = (held[p, at, :] * factor).astype(jnp.bfloat16)
            return carry

        lax.fori_loop(0, rows // chunk, body, 0)
        for k in range(1, n):
            row_copy(p, k, me, columns(j)).start()

    gain_copy = pltpu.make_async_copy(gain_hbm, gain, gain_sem)
    gain_copy.start()
    ahead = min(SLOTS, units)

    def begin(j, carry):
        for p in range(2):
            for copy in loads(j, p):
                copy.start()
        return carry

    lax.fori_loop(0, ahead // 2, begin, 0)

    barrier = pltpu.get_barrier_semaphore()
    for k in range(1, n):
        pl.semaphore_signal(barrier, inc=1, device_id={"rows": lax.rem(me + k, n)}, device_id_type=MESH)

    gain_copy.wait()
    for r in range(rows // LANES):
        spread = jnp.broadcast_to(gain[r : r + 1, :], (LANES, LANES)).T
        at = pl.ds(r * LANES, LANES)
        keep_scale[at, :] = spread * (1.0 - learn_rate * decay_rate)
        step_scale[at, :] = spread * learn_rate

    pl.semaphore_wait(barrier, n - 1)

    def refill(j, p):
        @pl.when(2 * j + p + ahead < units - 1)
        def _():
            for copy in loads(j + ahead // 2, p):
                copy.start()

        if p == (units - 1) % 2:

            @pl.when(2 * j + p + ahead == units - 1)
            def _():
                for c in range(rows // chunk):
                    for copy in piece_loads(c):
                        copy.start()

    def step(j, carry):
        update_shared(j, 0)
        refill(j, 0)

        @pl.when(j > 0)
        def _():
            finish(j - 1, 1)

        update_shared(j, 1)
        refill(j, 1)
        finish(j, 0)
        return carry

    lax.fori_loop(0, bulk // 2, step, 0)
    waiting = [bulk // 2 * 2 - 1]

    def finish_next():
        t = waiting.pop(0)
        (finish if t < bulk else finish_ready)(*unit_of(t))

    for t in range(bulk // 2 * 2, units):
        if t < whole:
            update_shared(*unit_of(t))
            waiting.append(t)
        else:
            update_rest(*unit_of(t), t - whole)
        if waiting and (waiting[0] < t):
            finish_next()
    while waiting:
        finish_next()

    for p in range(2):
        ended = pl.ds(0, (bulk + 1 - p) // 2 * SLAB)
        for k in range(1, n):
            row_copy(p, k, me, ended).wait_send()
            row_copy(p, k, lax.rem(me + n - k, n), ended).wait_recv()


def store_kernel(n, pieces, bulk, gate, up, ready, out_g, out_u, sem, ready_sem):
    height = gate.shape[0] // pieces
    rows = gate.shape[0] // n
    mine = pl.ds(pl.multiple_of(lax.axis_index("rows") * rows, rows), rows)
    ends = ((bulk + 1) // 2 * SLAB, bulk // 2 * SLAB)
    outs = (out_g, out_u)
    copies = []
    for p, source in enumerate((gate, up)):
        for i in range(pieces):
            at = (pl.ds(i * height, height), pl.ds(0, ends[p]))
            pltpu.make_async_copy(source.at[at], outs[p].at[at], sem.at[p]).start()
        at = (slice(None), pl.ds(0, ends[p]))
        copies.append(pltpu.make_async_copy(source.at[at], outs[p].at[at], sem.at[p]))
    for u in range(READY):
        j, p = unit_of(bulk + u)
        copies.append(
            pltpu.make_async_copy(ready.at[u], outs[p].at[mine, pl.ds(j * SLAB, SLAB)], ready_sem.at[u])
        )
        copies[-1].start()
    for copy in copies:
        copy.wait()


def rest_kernel(n, bulk, *refs):
    peers_ready, own, peers = refs[: n - 1], refs[n - 1], refs[n : 2 * n - 1]
    col_g, col_u, _, _, out_g, out_u, out_cg, out_cu, block, last, sem, ready_sem, col_sem, last_sem = refs[2 * n - 1 :]
    rows = own.shape[1] - 8
    chunk = min(rows, 256)
    whole = bulk + READY
    me = lax.axis_index("rows")
    outs, cols, out_cols = (out_g, out_u), (col_g, col_u), (out_cg, out_cu)
    copies = []

    def begin(source, target, semaphore):
        copies.append(pltpu.make_async_copy(source, target, semaphore))
        copies[-1].start()

    def place(k):
        return pl.ds(pl.multiple_of(lax.rem(me + n - k, n) * rows, rows), rows)

    for u in range(READY):
        j, p = unit_of(bulk + u)
        for k, peer in enumerate(peers_ready, 1):
            begin(peer.at[u], outs[p].at[place(k), pl.ds(j * SLAB, SLAB)], ready_sem.at[u, k - 1])
    for p in range(2):
        at = (slice(None), pl.ds(0, (whole + 1 - p) // 2 * SLAB))
        begin(cols[p].at[at], out_cols[p].at[at], col_sem.at[p])
    for u in range(REST):
        j, p = unit_of(whole + u)
        at_columns = pl.ds(j * SLAB, SLAB)
        total = own[u, pl.ds(rows, 8), :]
        for peer in peers:
            total = total + peer[u, pl.ds(rows, 8), :]
        mean = jnp.sum(total, axis=0, keepdims=True) / (n * rows)
        last[u] = mean
        begin(last.at[u], out_cols[p].at[:, at_columns], last_sem.at[u])
        factor = 1.0 / mean
        for k, source in enumerate((own, *peers)):
            owner = lax.rem(me + n - k, n)

            def body(c, carry):
                at = pl.ds(pl.multiple_of(c * chunk, chunk), chunk)
                to = pl.ds(pl.multiple_of(owner * rows + c * chunk, chunk), chunk)
                block[u, to, :] = (source[u, at, :] * factor).astype(jnp.bfloat16)
                return carry

            lax.fori_loop(0, rows // chunk, body, 0)
            begin(block.at[u, place(k)], outs[p].at[place(k), at_columns], sem.at[u, k])
    for copy in copies:
        copy.wait()


def solution(mesh):
    n = mesh.shape["rows"]

    def shards(weight_gate, moment_gate, square_gate, weight_up, moment_up, square_up, norm_gain):
        rows, width = weight_gate.shape
        units = 2 * (width // SLAB)
        bulk = units - REST - READY
        peers = max(n - 1, 1)
        any_space = pl.BlockSpec(memory_space=pl.ANY)
        in_vmem = pl.BlockSpec(memory_space=pltpu.VMEM)
        full = ((n * rows, width), jnp.bfloat16)
        column = ((1, width), jnp.float32)
        dma = pltpu.SemaphoreType.DMA
        gate, up, col_g, col_u, ready, rest = pl.pallas_call(
            functools.partial(exchange_kernel, n),
            out_shape=tuple(
                pltpu.VMEM(*shape)
                for shape in (
                    full, full, column, column,
                    ((READY, rows, SLAB), jnp.bfloat16), ((REST, rows + 8, SLAB), jnp.float32),
                )
            ),
            in_specs=[any_space] * 6 + [pl.BlockSpec(memory_space=pltpu.HBM)],
            out_specs=[in_vmem] * 6,
            scratch_shapes=[
                pltpu.VMEM((SLOTS, 3, rows, SLAB), jnp.float32),
                pltpu.VMEM((2, rows, SLAB), jnp.float32),
                pltpu.VMEM((rows // LANES, LANES), jnp.float32),
                pltpu.VMEM((rows, LANES), jnp.float32),
                pltpu.VMEM((rows, LANES), jnp.float32),
                pltpu.VMEM((units, n, 8, SLAB), jnp.float32),
                dma((SLOTS,)),
                dma((RING, peers)),
                dma((RING, peers)),
                dma((2, peers)),
                dma((2, peers)),
                dma,
                dma((rows // min(rows, 256),)),
            ],
            compiler_params=pltpu.CompilerParams(
                collective_id=0, has_side_effects=True, vmem_limit_bytes=36 * 1024 * 1024
            ),
            name="exchange",
        )(
            weight_gate, moment_gate, square_gate, weight_up, moment_up, square_up,
            norm_gain.reshape(rows // LANES, LANES),
        )

        def from_peers(own):
            return [lax.ppermute(own, "rows", [(i, (i + k) % n) for i in range(n)]) for k in range(1, n)]

        others = from_peers(rest)
        others_ready = from_peers(ready)
        pieces = 4
        out_g, out_u = pl.pallas_call(
            functools.partial(store_kernel, n, pieces, bulk),
            out_shape=(jax.ShapeDtypeStruct(*full),) * 2,
            in_specs=[in_vmem] * 3,
            out_specs=[any_space] * 2,
            scratch_shapes=[dma((2,)), dma((READY,))],
            compiler_params=pltpu.CompilerParams(vmem_limit_bytes=1024 * 1024),
            cost_estimate=pl.CostEstimate(flops=200_000_000, bytes_accessed=4 * n * rows * width, transcendentals=0),
            name="store",
        )(gate, up, ready)
        first = 2 * n + 1
        out_g, out_u, out_cg, out_cu = pl.pallas_call(
            functools.partial(rest_kernel, n, bulk),
            out_shape=(jax.ShapeDtypeStruct(*full),) * 2 + (jax.ShapeDtypeStruct(*column),) * 2,
            in_specs=[in_vmem] * first + [any_space] * 2,
            out_specs=[any_space] * 4,
            input_output_aliases={first: 0, first + 1: 1},
            scratch_shapes=[
                pltpu.VMEM((REST, n * rows, SLAB), jnp.bfloat16),
                pltpu.VMEM((REST, 1, SLAB), jnp.float32),
                dma((REST, n)),
                dma((READY, peers)),
                dma((2,)),
                dma((REST,)),
            ],
            compiler_params=pltpu.CompilerParams(vmem_limit_bytes=8 * 1024 * 1024),
            name="rest",
        )(*others_ready, rest, *others, col_g, col_u, out_g, out_u)
        return out_g, out_u, out_cg.reshape(width), out_cu.reshape(width)

    held = P(("trial", "rows"), "cols")
    return jax.shard_map(
        shards,
        mesh=mesh,
        in_specs=(held,) * 6 + (P(("trial", "rows")),),
        out_specs=(P("trial", "cols"), P("trial", "cols"), P(("trial", "cols")), P(("trial", "cols"))),
        check_vma=False,
    )
```

time: 25.9 us -> 25.1 us (0.969)
  Pallas kernels: 24.3 us -> 23.7 us
  waiting for transfers between devices: 0.32 us -> 0.01 us
    pallas_call x1, Pallas kernels: 17.5 us -> 17 us  [shards(): pl.pallas_call(functools.partial(exchange_kernel, n), out_shape=tuple((pl...]
    ppermute x1 -> x2, waiting for transfers between devices: 0.32 us -> 0.01 us  [from_peers(): lax.ppermute(own, 'rows', [(i, (i + k) % n) for i in range(n)])]
    ppermute x1 -> x2, starting transfers between devices: 0.47 us -> 0.58 us  [from_peers(): lax.ppermute(own, 'rows', [(i, (i + k) % n) for i in range(n)])]
  transfers between devices with their start and end apart: 1 -> 2, of which waited for: 1 -> 0; matrix products, arithmetic and copies ran while one was open for 0% -> 0% of each run, Pallas kernels for 19% -> 20%
where the time goes in v2:
time: 25.1 us; the launch traced here: 24.9 us
  Pallas kernels  23.7 us (94%)
  between operations  0.67 us (3%)
  starting transfers between devices  0.58 us (2%)
    pallas_call x1, Pallas kernels, shards(): pl.pallas_call(functools.partial(exchange_kernel, n), out_shape=tuple((pl...  17 us
    pallas_call x1, Pallas kernels, shards(): pl.pallas_call(functools.partial(store_kernel, n, pieces, bulk), out_shap...  5.07 us
    pallas_call x1, Pallas kernels, shards(): pl.pallas_call(functools.partial(rest_kernel, n, bulk), out_shape=(jax.Sh...  1.59 us
    ppermute x2, starting transfers between devices, from_peers(): lax.ppermute(own, 'rows', [(i, (i + k) % n) for i in range(n)])  0.58 us
  transfers between devices with their start and end apart: 2, of which 0 were waited for; matrix products, arithmetic and copies ran while one was open for 0% of the time, Pallas kernels for 20%

profile of v2, /device:TPU:3, one launch (start us, length us, event | category | flops | bytes accessed | tf_op | source)
XLA Modules:
  0.0 24.9 jit_solution(12777451071760694775)
XLA Ops:
  0.6 17.0 %exchange.1 = (bf16[2048,2048]{1,0:T(8,128)(2,1)S(1)}, bf16[2048,2048]{1,0:T(8,128)(2,1)S(1)}, f32[1,2048]{1,0:T(1,128)S(1)}, f32[1,2048]{1,0:T(1,128)S(1)}, bf1...) custom-call(f32[1024,2048]{1,0:T(8,128)} %wg.1, f32[1024,2048]{1,0:T(8,128)} %mg.1, f32[1024,2048]{1,0:T(8,128)} %sg.1, ...), custom_call_target="tpu_custom_call" | custom-call | tf_op jit(solution)/shard_map/exchange/pallas_call | solution.py:328
  17.6 0.3 %collective-permute-start.1 = (f32[2,1032,256]{2,1,0:T(8,128)S(1)}, f32[2,1032,256]{2,1,0:T(8,128)S(1)}, u32[]{:S(2)}, u32[]{:S(2)}) collective-permute-start(f32[2,1032,256]{2,1,0:T(8,128)S(1)} %get-tuple-element.17.refs_1_), channel_id=1, source_target_pairs={{0,4},{4,0},{1,5},{5,1},{2,6},{6,2},{3,7},{7,3},{8,12},{12,8},{9,1... | collective-permute-start | bytes 6340616 | tf_op jit(solution)/shard_map/ppermute | solution.py:364
  18.0 0.3 %collective-permute-start = (bf16[1,1024,256]{2,1,0:T(8,128)(2,1)S(1)}, bf16[1,1024,256]{2,1,0:T(8,128)(2,1)S(1)}, u32[]{:S(2)}, u32[]{:S(2)}) collective-permute-start(bf16[1,1024,256]{2,1,0:T(8,128)(2,1)S(1)} %get-tuple-element.16.ready), channel_id=1, source_target_pairs={{0,4},{4,0},{1,5},{5,1},{2,6},{6,2},{3,7},{7,3},{8,12},{12,8},{9,1... | collective-permute-start | bytes 1572872 | tf_op jit(solution)/shard_map/ppermute | solution.py:364
  18.2 5.1 %store.1 = (bf16[2048,2048]{1,0:T(8,128)(2,1)}, bf16[2048,2048]{1,0:T(8,128)(2,1)}) custom-call(bf16[2048,2048]{1,0:T(8,128)(2,1)S(1)} %get-tuple-element.20.gate, bf16[2048,2048]{1,0:T(8,128)(2,1)S(1)} %get-tuple-element.21.up, bf16[1,1024,256]{2,1,0:T(8,128)(2,1)S(1)} %get-tuple-element.16.ready), custom_call_target="tpu_custom_call" | custom-call | flops 200000000 | bytes 16777216 | tf_op jit(solution)/shard_map/store/pallas_call | solution.py:369
  23.3 0.0 collective-permute-done.refs_0_
  23.3 0.0 collective-permute-done.1.refs_2_
  23.3 1.6 %rest.1 = (bf16[2048,2048]{1,0:T(8,128)(2,1)}, bf16[2048,2048]{1,0:T(8,128)(2,1)}, f32[1,2048]{1,0:T(1,128)}, f32[1,2048]{1,0:T(1,128)}) custom-call(bf16[1,1024,256]{2,1,0:T(8,128)(2,1)S(1)} %collective-permute-done.refs_0_, f32[2,1032,256]{2,1,0:T(8,128)S(1)} %get-tuple-element.17.refs_1_, ...), custom_call_target="tpu_custom_call", output_to_operand_aliasing={{0}: (5, {}), {1}: (6, {})} | custom-call | tf_op jit(solution)/shard_map/rest/pallas_call | solution.py:380
Async XLA Ops:
  17.6 5.7 %collective-permute-start.1 = (f32[2,1032,256]{2,1,0:T(8,128)S(1)}, f32[2,1032,256]{2,1,0:T(8,128)S(1)}, u32[]{:S(2)}, u32[]{:S(2)}) collective-permute-start(f32[2,1032,256]{2,1,0:T(8,128)S(1)} %get-tuple-element.17.refs_1_), channel_id=1, source_target_pairs={{0,4},{4,0},{1,5},{5,1},{2,6},{6,2},{3,7},{7,3},{8,12},{12,8},{9,1... | collective-permute-start | bytes 6340616 | tf_op jit(solution)/shard_map/ppermute | solution.py:364
  18.0 5.3 %collective-permute-start = (bf16[1,1024,256]{2,1,0:T(8,128)(2,1)S(1)}, bf16[1,1024,256]{2,1,0:T(8,128)(2,1)S(1)}, u32[]{:S(2)}, u32[]{:S(2)}) collective-permute-start(bf16[1,1024,256]{2,1,0:T(8,128)(2,1)S(1)} %get-tuple-element.16.ready), channel_id=1, source_target_pairs={{0,4},{4,0},{1,5},{5,1},{2,6},{6,2},{3,7},{7,3},{8,12},{12,8},{9,1... | collective-permute-start | bytes 1572872 | tf_op jit(solution)/shard_map/ppermute | solution.py:364

commit v3 on v2

--- a/solution.py
+++ b/solution.py
@@ -24,10 +24,15 @@
     return t // 2, t % 2
 
 
+def halves(value):
+    high = value.astype(jnp.bfloat16)
+    return high, (value - high.astype(jnp.float32)).astype(jnp.bfloat16)
+
+
 def exchange_kernel(
-    n, wg, mg, sg, wu, mu, su, gain_hbm, out_g, out_u, col_g, col_u, ready, rest,
+    n, wg, mg, sg, wu, mu, su, gain_hbm, out_g, out_u, col_g, col_u, parcel,
     buf, held, gain, keep_scale, step_scale, parts,
-    in_sem, part_send, part_recv, row_send, row_recv, gain_sem, piece_sem,
+    in_sem, part_send, part_recv, row_send, row_recv, piece_sem,
 ):
     rows, width = wg.shape
     units = 2 * (width // SLAB)
@@ -69,7 +74,7 @@
         return pltpu.make_async_remote_copy(
             src_ref=parts.at[t, owner],
             dst_ref=parts.at[t, owner],
-            send_sem=part_send.at[lax.rem(t, RING), k - 1],
+            send_sem=part_send.at[lax.rem(t, 2), k - 1],
             recv_sem=part_recv.at[lax.rem(t, RING), k - 1],
             device_id={"rows": lax.rem(me + k, n)},
             device_id_type=MESH,
@@ -121,12 +126,19 @@
             part_copy(j, p, k, me).start()
 
     def update_rest(j, p, u):
+        high, low = READY + 2 * u, READY + 2 * u + 1
+
         def keep_value(at, tile, value):
-            rest[u, at, tile] = value
+            parcel[high, at, tile], parcel[low, at, tile] = halves(value)
 
         sums = update(j, p, keep_value, pieces=2 * j + p == units - 1)
+        tail = pl.ds(rows, 16)
         for i in range(SLAB // LANES):
-            rest[u, pl.ds(rows, 8), pl.ds(i * LANES, LANES)] = sums[i]
+            lanes = pl.ds(i * LANES, LANES)
+            first, second = halves(sums[i])
+            third = sums[i] - first.astype(jnp.float32) - second.astype(jnp.float32)
+            parcel[high, tail, lanes] = jnp.concatenate([first.astype(jnp.float32), second.astype(jnp.float32)]).astype(jnp.bfloat16)
+            parcel[low, tail, lanes] = jnp.concatenate([third, zero]).astype(jnp.bfloat16)
 
     def factor_of(j, p):
         t = 2 * j + p
@@ -145,7 +157,7 @@
 
         def body(c, carry):
             at = pl.ds(pl.multiple_of(c * chunk, chunk), chunk)
-            ready[2 * j + p - bulk, at, :] = (held[p, at, :] * factor).astype(jnp.bfloat16)
+            parcel[2 * j + p - bulk, at, :] = (held[p, at, :] * factor).astype(jnp.bfloat16)
             return carry
 
         lax.fori_loop(0, rows // chunk, body, 0)
@@ -163,7 +175,7 @@
         for k in range(1, n):
             row_copy(p, k, me, columns(j)).start()
 
-    gain_copy = pltpu.make_async_copy(gain_hbm, gain, gain_sem)
+    gain_copy = pltpu.make_async_copy(gain_hbm, gain, piece_sem.at[0])
     gain_copy.start()
     ahead = min(SLOTS, units)
 
@@ -240,7 +252,7 @@
             row_copy(p, k, lax.rem(me + n - k, n), ended).wait_recv()
 
 
-def store_kernel(n, pieces, bulk, gate, up, ready, out_g, out_u, sem, ready_sem):
+def store_kernel(n, pieces, bulk, gate, up, parcel, out_g, out_u, sem, ready_sem):
     height = gate.shape[0] // pieces
     rows = gate.shape[0] // n
     mine = pl.ds(pl.multiple_of(lax.axis_index("rows") * rows, rows), rows)
@@ -256,7 +268,7 @@
     for u in range(READY):
         j, p = unit_of(bulk + u)
         copies.append(
-            pltpu.make_async_copy(ready.at[u], outs[p].at[mine, pl.ds(j * SLAB, SLAB)], ready_sem.at[u])
+            pltpu.make_async_copy(parcel.at[u, pl.ds(0, rows)], outs[p].at[mine, pl.ds(j * SLAB, SLAB)], ready_sem.at[u])
         )
         copies[-1].start()
     for copy in copies:
@@ -264,38 +276,41 @@
 
 
 def rest_kernel(n, bulk, *refs):
-    peers_ready, own, peers = refs[: n - 1], refs[n - 1], refs[n : 2 * n - 1]
-    col_g, col_u, _, _, out_g, out_u, out_cg, out_cu, block, last, sem, ready_sem, col_sem, last_sem = refs[2 * n - 1 :]
-    rows = own.shape[1] - 8
+    own, peers = refs[0], refs[1:n]
+    col_g, col_u, _, _, out_g, out_u, out_cg, out_cu, block, last, sem, ready_sem, col_sem = refs[n:]
+    rows = own.shape[1] - 16
     chunk = min(rows, 256)
     whole = bulk + READY
     me = lax.axis_index("rows")
     outs, cols, out_cols = (out_g, out_u), (col_g, col_u), (out_cg, out_cu)
-    copies = []
-
     def begin(source, target, semaphore):
-        copies.append(pltpu.make_async_copy(source, target, semaphore))
-        copies[-1].start()
+        pltpu.make_async_copy(source, target, semaphore).start()
+
+    def end(target, semaphore):
+        pltpu.make_async_copy(target, target, semaphore).wait()
 
     def place(k):
         return pl.ds(pl.multiple_of(lax.rem(me + n - k, n) * rows, rows), rows)
 
     for u in range(READY):
         j, p = unit_of(bulk + u)
-        for k, peer in enumerate(peers_ready, 1):
-            begin(peer.at[u], outs[p].at[place(k), pl.ds(j * SLAB, SLAB)], ready_sem.at[u, k - 1])
+        for k, peer in enumerate(peers, 1):
+            begin(peer.at[u, pl.ds(0, rows)], outs[p].at[place(k), pl.ds(j * SLAB, SLAB)], ready_sem.at[u])
     for p in range(2):
         at = (slice(None), pl.ds(0, (whole + 1 - p) // 2 * SLAB))
         begin(cols[p].at[at], out_cols[p].at[at], col_sem.at[p])
     for u in range(REST):
         j, p = unit_of(whole + u)
         at_columns = pl.ds(j * SLAB, SLAB)
-        total = own[u, pl.ds(rows, 8), :]
-        for peer in peers:
-            total = total + peer[u, pl.ds(rows, 8), :]
+        high, low = READY + 2 * u, READY + 2 * u + 1
+        total = jnp.zeros((8, SLAB), jnp.float32)
+        for source in (own, *peers):
+            upper = source[high, pl.ds(rows, 16), :].astype(jnp.float32)
+            lower = source[low, pl.ds(rows, 16), :].astype(jnp.float32)
+            total = total + (upper[:8] + upper[8:] + lower[:8])
         mean = jnp.sum(total, axis=0, keepdims=True) / (n * rows)
         last[u] = mean
-        begin(last.at[u], out_cols[p].at[:, at_columns], last_sem.at[u])
+        begin(last.at[u], out_cols[p].at[:, at_columns], col_sem.at[p])
         factor = 1.0 / mean
         for k, source in enumerate((own, *peers)):
             owner = lax.rem(me + n - k, n)
@@ -303,13 +318,21 @@
             def body(c, carry):
                 at = pl.ds(pl.multiple_of(c * chunk, chunk), chunk)
                 to = pl.ds(pl.multiple_of(owner * rows + c * chunk, chunk), chunk)
-                block[u, to, :] = (source[u, at, :] * factor).astype(jnp.bfloat16)
+                value = source[high, at, :].astype(jnp.float32) + source[low, at, :].astype(jnp.float32)
+                block[u, to, :] = (value * factor).astype(jnp.bfloat16)
                 return carry
 
             lax.fori_loop(0, rows // chunk, body, 0)
-            begin(block.at[u, place(k)], outs[p].at[place(k), at_columns], sem.at[u, k])
-    for copy in copies:
-        copy.wait()
+            begin(block.at[u, place(k)], outs[p].at[place(k), at_columns], sem.at[u])
+    for u in range(READY):
+        j, p = unit_of(bulk + u)
+        if n > 1:
+            end(outs[p].at[pl.ds(0, (n - 1) * rows), pl.ds(j * SLAB, SLAB)], ready_sem.at[u])
+    for u in range(REST):
+        j, p = unit_of(whole + u)
+        end(outs[p].at[:, pl.ds(j * SLAB, SLAB)], sem.at[u])
+    for p in range(2):
+        end(out_cols[p], col_sem.at[p])
 
 
 def solution(mesh):
@@ -325,17 +348,17 @@
         full = ((n * rows, width), jnp.bfloat16)
         column = ((1, width), jnp.float32)
         dma = pltpu.SemaphoreType.DMA
-        gate, up, col_g, col_u, ready, rest = pl.pallas_call(
+        gate, up, col_g, col_u, parcel = pl.pallas_call(
             functools.partial(exchange_kernel, n),
             out_shape=tuple(
                 pltpu.VMEM(*shape)
                 for shape in (
                     full, full, column, column,
-                    ((READY, rows, SLAB), jnp.bfloat16), ((REST, rows + 8, SLAB), jnp.float32),
+                    ((READY + 2 * REST, rows + 16, SLAB), jnp.bfloat16),
                 )
             ),
             in_specs=[any_space] * 6 + [pl.BlockSpec(memory_space=pltpu.HBM)],
-            out_specs=[in_vmem] * 6,
+            out_specs=[in_vmem] * 5,
             scratch_shapes=[
                 pltpu.VMEM((SLOTS, 3, rows, SLAB), jnp.float32),
                 pltpu.VMEM((2, rows, SLAB), jnp.float32),
@@ -344,11 +367,10 @@
                 pltpu.VMEM((rows, LANES), jnp.float32),
                 pltpu.VMEM((units, n, 8, SLAB), jnp.float32),
                 dma((SLOTS,)),
-                dma((RING, peers)),
+                dma((2, peers)),
                 dma((RING, peers)),
                 dma((2, peers)),
                 dma((2, peers)),
-                dma,
                 dma((rows // min(rows, 256),)),
             ],
             compiler_params=pltpu.CompilerParams(
@@ -360,11 +382,9 @@
             norm_gain.reshape(rows // LANES, LANES),
         )
 
-        def from_peers(own):
-            return [lax.ppermute(own, "rows", [(i, (i + k) % n) for i in range(n)]) for k in range(1, n)]
-
-        others = from_peers(rest)
-        others_ready = from_peers(ready)
+        others = [
+            lax.ppermute(parcel, "rows", [(i, (i + k) % n) for i in range(n)]) for k in range(1, n)
+        ]
         pieces = 4
         out_g, out_u = pl.pallas_call(
             functools.partial(store_kernel, n, pieces, bulk),
@@ -375,8 +395,8 @@
             compiler_params=pltpu.CompilerParams(vmem_limit_bytes=1024 * 1024),
             cost_estimate=pl.CostEstimate(flops=200_000_000, bytes_accessed=4 * n * rows * width, transcendentals=0),
             name="store",
-        )(gate, up, ready)
-        first = 2 * n + 1
+        )(gate, up, parcel)
+        first = n + 2
         out_g, out_u, out_cg, out_cu = pl.pallas_call(
             functools.partial(rest_kernel, n, bulk),
             out_shape=(jax.ShapeDtypeStruct(*full),) * 2 + (jax.ShapeDtypeStruct(*column),) * 2,
@@ -386,14 +406,13 @@
             scratch_shapes=[
                 pltpu.VMEM((REST, n * rows, SLAB), jnp.bfloat16),
                 pltpu.VMEM((REST, 1, SLAB), jnp.float32),
-                dma((REST, n)),
-                dma((READY, peers)),
+                dma((REST,)),
+                dma((READY,)),
                 dma((2,)),
-                dma((REST,)),
             ],
             compiler_params=pltpu.CompilerParams(vmem_limit_bytes=8 * 1024 * 1024),
             name="rest",
-        )(*others_ready, rest, *others, col_g, col_u, out_g, out_u)
+        )(parcel, *others, col_g, col_u, out_g, out_u)
         return out_g, out_u, out_cg.reshape(width), out_cu.reshape(width)
 
     held = P(("trial", "rows"), "cols")

time: 25.1 us -> 24.8 us (0.988)
    ppermute x2 -> x1, starting transfers between devices: 0.58 us -> 0.4 us  [shards(): lax.ppermute(parcel, 'rows', [(i, (i + k) % n) for i in range(n)])]
  transfers between devices with their start and end apart: 2 -> 1, of which waited for: 0 -> 0; matrix products, arithmetic and copies ran while one was open for 0% -> 0% of each run, Pallas kernels for 20% -> 21%
where the time goes in v3:
time: 24.8 us; the launch traced here: 24.7 us
  Pallas kernels  23.6 us (95%)
  between operations  0.66 us (3%)
  starting transfers between devices  0.4 us (2%)
    pallas_call x1, Pallas kernels, shards(): pl.pallas_call(functools.partial(exchange_kernel, n), out_shape=tuple((pl...  17 us
    pallas_call x1, Pallas kernels, shards(): pl.pallas_call(functools.partial(store_kernel, n, pieces, bulk), out_shap...  5.07 us
    pallas_call x1, Pallas kernels, shards(): pl.pallas_call(functools.partial(rest_kernel, n, bulk), out_shape=(jax.Sh...  1.57 us
  transfers between devices with their start and end apart: 1, of which 0 were waited for; matrix products, arithmetic and copies ran while one was open for 0% of the time, Pallas kernels for 21%

profile of v3, /device:TPU:3, one launch (start us, length us, event | category | flops | bytes accessed | tf_op | source)
XLA Modules:
  0.0 24.7 jit_solution(12121778300377651906)
XLA Ops:
  0.6 17.0 %exchange.1 = (bf16[2048,2048]{1,0:T(8,128)(2,1)S(1)}, bf16[2048,2048]{1,0:T(8,128)(2,1)S(1)}, f32[1,2048]{1,0:T(1,128)S(1)}, f32[1,2048]{1,0:T(1,128)S(1)}, bf16[5,1040,256]{2,1,0:T(8,128)(2,1)S(1)}) custom-call(f32[1024,2048]{1,0:T(8,128)} %wg.1, f32[1024,2048]{1,0:T(8,128)} %mg.1, f32[1024,2048]{1,0:T(8,128)} %sg.1, f32[1024,2048]{1,0:T(8,128)} %wu.1, ...), custom_call_target="tpu_custom_call" | custom-call | tf_op jit(solution)/shard_map/exchange/pallas_call | solution.py:351
  17.6 0.4 %collective-permute-start = (bf16[5,1040,256]{2,1,0:T(8,128)(2,1)S(1)}, bf16[5,1040,256]{2,1,0:T(8,128)(2,1)S(1)}, u32[]{:S(2)}, u32[]{:S(2)}) collective-permute-start(bf16[5,1040,256]{2,1,0:T(8,128)(2,1)S(1)} %get-tuple-element.15.parcel.refs_0_), channel_id=1, source_target_pairs={{0,4},{4,0},{1,5},{5,1},{2,6},{6,2},{3,7},{7,3},{8,12},{12,8},{9,1... | collective-permute-start | bytes 7987208 | tf_op jit(solution)/shard_map/ppermute | solution.py:386
  18.0 5.1 %store.1 = (bf16[2048,2048]{1,0:T(8,128)(2,1)}, bf16[2048,2048]{1,0:T(8,128)(2,1)}) custom-call(bf16[2048,2048]{1,0:T(8,128)(2,1)S(1)} %get-tuple-element.18.gate, bf16[2048,2048]{1,0:T(8,128)(2,1)S(1)} %get-tuple-element.19.up, bf16[5,1040,256]{2,1,0:T(8,128)(2,1)S(1)} %get-tuple-element.15.parcel.refs_0_), custom_call_target="tpu_custom_call" | custom-call | flops 200000000 | bytes 16777216 | tf_op jit(solution)/shard_map/store/pallas_call | solution.py:389
  23.1 0.0 collective-permute-done.refs_1_
  23.1 1.6 %rest.1 = (bf16[2048,2048]{1,0:T(8,128)(2,1)}, bf16[2048,2048]{1,0:T(8,128)(2,1)}, f32[1,2048]{1,0:T(1,128)}, f32[1,2048]{1,0:T(1,128)}) custom-call(bf16[5,1040,256]{2,1,0:T(8,128)(2,1)S(1)} %get-tuple-element.15.parcel.refs_0_, bf16[5,1040,256]{2,1,0:T(8,128)(2,1)S(1)} %collective-permute-done.refs_1_, ...), custom_call_target="tpu_custom_call", output_to_operand_aliasing={{0}: (4, {}), {1}: (5, {})} | custom-call | tf_op jit(solution)/shard_map/rest/pallas_call | solution.py:400
Async XLA Ops:
  17.6 5.5 %collective-permute-start = (bf16[5,1040,256]{2,1,0:T(8,128)(2,1)S(1)}, bf16[5,1040,256]{2,1,0:T(8,128)(2,1)S(1)}, u32[]{:S(2)}, u32[]{:S(2)}) collective-permute-start(bf16[5,1040,256]{2,1,0:T(8,128)(2,1)S(1)} %get-tuple-element.15.parcel.refs_0_), channel_id=1, source_target_pairs={{0,4},{4,0},{1,5},{5,1},{2,6},{6,2},{3,7},{7,3},{8,12},{12,8},{9,1... | collective-permute-start | bytes 7987208 | tf_op jit(solution)/shard_map/ppermute | solution.py:386

commit v4 on v3

--- a/solution.py
+++ b/solution.py
@@ -80,8 +80,9 @@
             device_id_type=MESH,
         )
 
-    def row_copy(p, k, owner, at_columns):
-        block = outs[p].at[pl.ds(pl.multiple_of(owner * rows, rows), rows), at_columns]
+    def row_copy(p, k, owner, at_columns, c=0, height=None):
+        height = height or rows
+        block = outs[p].at[pl.ds(pl.multiple_of(owner * rows + c * height, height), height), at_columns]
         return pltpu.make_async_remote_copy(
             src_ref=block,
             dst_ref=block,
@@ -169,11 +170,11 @@
             at = pl.ds(pl.multiple_of(c * chunk, chunk), chunk)
             to = pl.ds(pl.multiple_of(me * rows + c * chunk, chunk), chunk)
             outs[p][to, columns(j)] = (held[p, at, :] * factor).astype(jnp.bfloat16)
+            for k in range(1, n):
+                row_copy(p, k, me, columns(j), c, chunk).start()
             return carry
 
         lax.fori_loop(0, rows // chunk, body, 0)
-        for k in range(1, n):
-            row_copy(p, k, me, columns(j)).start()
 
     gain_copy = pltpu.make_async_copy(gain_hbm, gain, piece_sem.at[0])
     gain_copy.start()

time: 24.8 us -> 24.8 us (level)
  no operation moved by 1% of the time
where the time goes in v4:
time: 24.8 us; the launch traced here: 24.7 us
  Pallas kernels  23.5 us (95%)
  between operations  0.66 us (3%)
  starting transfers between devices  0.47 us (2%)
    pallas_call x1, Pallas kernels, shards(): pl.pallas_call(functools.partial(exchange_kernel, n), out_shape=tuple((pl...  16.9 us
    pallas_call x1, Pallas kernels, shards(): pl.pallas_call(functools.partial(store_kernel, n, pieces, bulk), out_shap...  5.07 us
    pallas_call x1, Pallas kernels, shards(): pl.pallas_call(functools.partial(rest_kernel, n, bulk), out_shape=(jax.Sh...  1.57 us
  transfers between devices with their start and end apart: 1, of which 0 were waited for; matrix products, arithmetic and copies ran while one was open for 0% of the time, Pallas kernels for 21%

profile of v4, /device:TPU:3, one launch (start us, length us, event | category | flops | bytes accessed | tf_op | source)
XLA Modules:
  0.0 24.7 jit_solution(3676081580197161634)
XLA Ops:
  0.6 16.9 %exchange.1 = (bf16[2048,2048]{1,0:T(8,128)(2,1)S(1)}, bf16[2048,2048]{1,0:T(8,128)(2,1)S(1)}, f32[1,2048]{1,0:T(1,128)S(1)}, f32[1,2048]{1,0:T(1,128)S(1)}, bf16[5,1040,256]{2,1,0:T(8,128)(2,1)S(1)}) custom-call(f32[1024,2048]{1,0:T(8,128)} %wg.1, f32[1024,2048]{1,0:T(8,128)} %mg.1, f32[1024,2048]{1,0:T(8,128)} %sg.1, f32[1024,2048]{1,0:T(8,128)} %wu.1, ...), custom_call_target="tpu_custom_call" | custom-call | tf_op jit(solution)/shard_map/exchange/pallas_call | solution.py:352
  17.5 0.5 %collective-permute-start = (bf16[5,1040,256]{2,1,0:T(8,128)(2,1)S(1)}, bf16[5,1040,256]{2,1,0:T(8,128)(2,1)S(1)}, u32[]{:S(2)}, u32[]{:S(2)}) collective-permute-start(bf16[5,1040,256]{2,1,0:T(8,128)(2,1)S(1)} %get-tuple-element.15.parcel.refs_0_), channel_id=1, source_target_pairs={{0,4},{4,0},{1,5},{5,1},{2,6},{6,2},{3,7},{7,3},{8,12},{12,8},{9,1... | collective-permute-start | bytes 7987208 | tf_op jit(solution)/shard_map/ppermute | solution.py:387
  18.0 5.1 %store.1 = (bf16[2048,2048]{1,0:T(8,128)(2,1)}, bf16[2048,2048]{1,0:T(8,128)(2,1)}) custom-call(bf16[2048,2048]{1,0:T(8,128)(2,1)S(1)} %get-tuple-element.18.gate, bf16[2048,2048]{1,0:T(8,128)(2,1)S(1)} %get-tuple-element.19.up, bf16[5,1040,256]{2,1,0:T(8,128)(2,1)S(1)} %get-tuple-element.15.parcel.refs_0_), custom_call_target="tpu_custom_call" | custom-call | flops 200000000 | bytes 16777216 | tf_op jit(solution)/shard_map/store/pallas_call | solution.py:390
  23.1 0.0 collective-permute-done.refs_1_
  23.1 1.6 %rest.1 = (bf16[2048,2048]{1,0:T(8,128)(2,1)}, bf16[2048,2048]{1,0:T(8,128)(2,1)}, f32[1,2048]{1,0:T(1,128)}, f32[1,2048]{1,0:T(1,128)}) custom-call(bf16[5,1040,256]{2,1,0:T(8,128)(2,1)S(1)} %get-tuple-element.15.parcel.refs_0_, bf16[5,1040,256]{2,1,0:T(8,128)(2,1)S(1)} %collective-permute-done.refs_1_, ...), custom_call_target="tpu_custom_call", output_to_operand_aliasing={{0}: (4, {}), {1}: (5, {})} | custom-call | tf_op jit(solution)/shard_map/rest/pallas_call | solution.py:401
Async XLA Ops:
  17.5 5.5 %collective-permute-start = (bf16[5,1040,256]{2,1,0:T(8,128)(2,1)S(1)}, bf16[5,1040,256]{2,1,0:T(8,128)(2,1)S(1)}, u32[]{:S(2)}, u32[]{:S(2)}) collective-permute-start(bf16[5,1040,256]{2,1,0:T(8,128)(2,1)S(1)} %get-tuple-element.15.parcel.refs_0_), channel_id=1, source_target_pairs={{0,4},{4,0},{1,5},{5,1},{2,6},{6,2},{3,7},{7,3},{8,12},{12,8},{9,1... | collective-permute-start | bytes 7987208 | tf_op jit(solution)/shard_map/ppermute | solution.py:387
